TPU v7x, 32 devices: a whole 2x2x4 slice. The times are simulated.
32 devices in a mesh: row: 16 (over z, x, core), ch: 2 (over y).
Axes of the slice: x: 2, y: 2, z: 4, core: 2. Of those that a mesh axis runs over, the one named last changes fastest.
Arguments:
- pair_rep: float32 [256, 256, 128], P('row', 'ch'), may hold values from -6 to 6
- residue_mask: int32 [256], replicated, may hold values 0 or 1
- pair_gain: float32 [2, 128], replicated, may hold values from 0.5 to 1.5
- pair_shift: float32 [2, 128], replicated, may hold values from -3 to 3
- panel_weight: bfloat16 [2, 128, 512], replicated, may hold values from -0.5 to 0.5
- panel_bias: float32 [2, 512], replicated, may hold values from -3 to 3
- gate_weight: bfloat16 [2, 128, 128], replicated, may hold values from -0.5 to 0.5
- gate_bias: float32 [2, 128], replicated, may hold values from -3 to 3
- hidden_gain: float32 [2, 128], replicated, may hold values from 0.5 to 1.5
- hidden_shift: float32 [2, 128], replicated, may hold values from -3 to 3
- output_weight: bfloat16 [2, 128, 128], replicated, may hold values from -0.5 to 0.5
- output_bias: float32 [2, 128], replicated, may hold values from -3 to 3
Outputs:
- updated_pair: float32 [256, 256, 128], P('row', 'ch')
All inputs are finite; a program needn't handle non-finite values.
Results may differ from a plain program's by a relative error of at most 0.0039.
Values may be sent and summed in bfloat16 or wider, within the bound.
A program may use at most 64 MiB of HBM per device.

v0:
```python
import jax
import jax.numpy as jnp
from jax import lax
from jax.sharding import PartitionSpec as P

PAIR_EPSILON = 1e-05
HIDDEN_EPSILON = 1.0


def layer_norm(values, gain_value, shift_value, along, epsilon):
    center = jnp.mean(values, axis=along, keepdims=True)
    offset = values - center
    spread = jnp.mean(offset * offset, axis=along, keepdims=True)
    return offset * lax.rsqrt(spread + epsilon) * gain_value + shift_value


def project(
    current,
    cell_mask,
    section_index,
    pair_gain,
    pair_shift,
    panel_weight,
    panel_bias,
    gate_weight,
    gate_bias,
):
    normed = layer_norm(
        current, pair_gain[section_index], pair_shift[section_index], 2, PAIR_EPSILON
    ).astype(jnp.bfloat16)
    hidden_width = panel_weight.shape[2] // 4
    features = jnp.einsum(
        "rjc,cf->frj", normed, panel_weight[section_index], preferred_element_type=jnp.float32
    )
    features = features + panel_bias[section_index][:, None, None]
    left_panel = (
        cell_mask
        * jax.nn.sigmoid(features[:hidden_width])
        * features[hidden_width : 2 * hidden_width]
    ).astype(jnp.bfloat16)
    right_panel = (
        cell_mask
        * jax.nn.sigmoid(features[2 * hidden_width : 3 * hidden_width])
        * features[3 * hidden_width :]
    ).astype(jnp.bfloat16)
    gate_value = jax.nn.sigmoid(
        jnp.einsum(
            "rjc,cd->rjd", normed, gate_weight[section_index], preferred_element_type=jnp.float32
        )
        + gate_bias[section_index]
    )
    return (left_panel, right_panel, gate_value)


def local(
    pair_rep,
    residue_mask,
    pair_gain,
    pair_shift,
    panel_weight,
    panel_bias,
    gate_weight,
    gate_bias,
    hidden_gain,
    hidden_shift,
    output_weight,
    output_bias,
):
    row_count = pair_rep.shape[0]
    col_count = pair_rep.shape[1]
    hidden_width = panel_weight.shape[2] // 4
    row_total = lax.axis_size("row")
    col_total = lax.axis_size("ch")
    group = hidden_width // col_total
    if group >= row_total:
        per_slot = group // row_total
        quarters = 1
    else:
        per_slot = 1
        quarters = row_total // group
    slots = row_total // quarters
    sub_rows = row_count // quarters
    blocks = col_count // row_count
    row_index = lax.axis_index("row")
    col_index = lax.axis_index("ch")
    residue_float = residue_mask.astype(jnp.float32)
    row_mask = lax.dynamic_slice_in_dim(residue_float, row_index * row_count, row_count)
    col_mask = lax.dynamic_slice_in_dim(residue_float, col_index * col_count, col_count)
    cell_mask = row_mask[:, None] * col_mask[None, :]
    current = pair_rep
    for section_index in range(2):
        left_panel, right_panel, gate_value = project(
            current,
            cell_mask,
            section_index,
            pair_gain,
            pair_shift,
            panel_weight,
            panel_bias,
            gate_weight,
            gate_bias,
        )
        if section_index == 0:
            send_left = left_panel.reshape(
                col_total, slots, per_slot, quarters, sub_rows, col_count
            )
            send_left = jnp.transpose(send_left, (0, 1, 3, 2, 4, 5)).reshape(
                col_total, row_total, per_slot, sub_rows, col_count
            )
        else:
            send_left = left_panel.reshape(
                col_total, slots, per_slot, row_count, blocks, quarters, sub_rows
            )
            send_left = jnp.transpose(send_left, (0, 1, 5, 2, 3, 4, 6)).reshape(
                col_total, row_total, per_slot, row_count, blocks * sub_rows
            )
        send_right = right_panel.reshape(col_total, slots, 1, per_slot, row_count, col_count)
        send_right = jnp.broadcast_to(
            send_right, (col_total, slots, quarters, per_slot, row_count, col_count)
        ).reshape(col_total, row_total, per_slot, row_count, col_count)
        got_left, got_right = (
            lax.all_to_all(
                lax.all_to_all(send_left, "ch", split_axis=0, concat_axis=4, tiled=True),
                "row",
                split_axis=1,
                concat_axis=3,
                tiled=True,
            ),
            lax.all_to_all(
                lax.all_to_all(send_right, "ch", split_axis=0, concat_axis=4, tiled=True),
                "row",
                split_axis=1,
                concat_axis=3,
                tiled=True,
            ),
        )
        got_left = got_left[0, 0]
        got_right = got_right[0, 0]
        if section_index == 0:
            products = jnp.einsum(
                "hik,hjk->hij", got_left, got_right, preferred_element_type=jnp.float32
            )
        else:
            products = jnp.einsum(
                "hki,hkj->hij", got_left, got_right, preferred_element_type=jnp.float32
            )
        returned = products.reshape(per_slot, row_total, sub_rows, col_total, col_count)
        gathered = lax.all_to_all(
            lax.all_to_all(returned, "row", split_axis=1, concat_axis=0, tiled=True),
            "ch",
            split_axis=3,
            concat_axis=0,
            tiled=True,
        )
        gathered = gathered.reshape(col_total, slots, quarters, per_slot, sub_rows, col_count)
        gathered = jnp.transpose(gathered, (0, 1, 3, 2, 4, 5)).reshape(
            hidden_width, row_count, col_count
        )
        normed = layer_norm(
            gathered,
            hidden_gain[section_index][:, None, None],
            hidden_shift[section_index][:, None, None],
            0,
            HIDDEN_EPSILON,
        ).astype(jnp.bfloat16)
        projected = jnp.einsum(
            "hrj,hc->rjc", normed, output_weight[section_index], preferred_element_type=jnp.float32
        )
        current = current + gate_value * (projected + output_bias[section_index])
    return current


def solution(mesh):
    return jax.shard_map(
        local,
        mesh=mesh,
        in_specs=(P("row", "ch", None), P(), P(), P(), P(), P(), P(), P(), P(), P(), P(), P()),
        out_specs=P("row", "ch", None),
        check_vma=False,
    )
```

profile of v0, /device:TPU:0, one launch (start us, length us, event | category | flops | bytes accessed | tf_op | source)
XLA Modules:
  0.0 238.2 jit_solution(15132575258035576822)
XLA Ops:
  0.8 1.6 reduce_sum.72
  2.4 1.9 multiply_reduce_fusion.3
  6.7 2.1 add_bitcast_fusion.1
  9.4 1.2 copy.82
  10.6 4.3 %all-to-all-start = ((bf16[2,16,4,16,128]{4,3,2,1,0:T(8,128)(2,1)}), bf16[2,16,4,16,128]{4,3,2,1,0:T(8,128)(2,1)S(1)}, u32[]{:S(2)}, u32[]{:S(2)}) async-start(bf16[2,16,4,16,128]{4,3,2,1,0:T(8,128)(2,1)} %bitcast.9), calls=%async_computation | async-start | bytes 1048576 | tf_op jit(solution)/shard_map/all_to_all | solution.py:123
  14.9 1.2 copy.86
  16.0 7.5 %all-to-all-done = bf16[2,16,4,16,128]{4,3,2,1,0:T(8,128)(2,1)S(1)} async-done(((bf16[2,16,4,16,128]{4,3,2,1,0:T(8,128)(2,1)}), bf16[2,16,4,16,128]{4,3,2,1,0:T(8,128)(2,1)S(1)}, u32[]{:S(2)}, u32[]{:S(2)}) %all-to-all-start) | async-done | bytes 524320 | tf_op jit(solution)/shard_map/all_to_all | solution.py:123
  23.6 3.5 %all-to-all-start.2 = ((bf16[2,16,4,16,128]{4,3,2,1,0:T(8,128)(2,1)}), bf16[2,16,4,16,128]{4,3,2,1,0:T(8,128)(2,1)S(1)}, u32[]{:S(2)}, u32[]{:S(2)}) async-start(bf16[2,16,4,16,128]{4,3,2,1,0:T(8,128)(2,1)} %bitcast.16), calls=%async_computation.2 | async-start | bytes 1048576 | tf_op jit(solution)/shard_map/all_to_all | solution.py:130
  28.0 6.8 %all-to-all-done.2 = bf16[2,16,4,16,128]{4,3,2,1,0:T(8,128)(2,1)S(1)} async-done(((bf16[2,16,4,16,128]{4,3,2,1,0:T(8,128)(2,1)}), bf16[2,16,4,16,128]{4,3,2,1,0:T(8,128)(2,1)S(1)}, u32[]{:S(2)}, u32[]{:S(2)}) %all-to-all-start.2) | async-done | bytes 524320 | tf_op jit(solution)/shard_map/all_to_all | solution.py:130
  34.7 5.9 %all-to-all-start.1 = ((bf16[1,16,4,16,256]{4,3,2,0,1:T(8,128)(2,1)}), bf16[1,16,4,16,256]{4,3,2,0,1:T(8,128)(2,1)S(1)}, u32[]{:S(2)}, u32[]{:S(2)}) async-start(bf16[1,16,4,16,256]{4,3,2,0,1:T(8,128)(2,1)} %bitcast_bitcast_fusion.3), calls=%async_computation.1 | async-start | bytes 1048576 | tf_op jit(solution)/shard_map/all_to_all | solution.py:122
  41.5 13.4 %all-to-all-done.1 = bf16[1,16,4,16,256]{4,3,2,0,1:T(8,128)(2,1)S(1)} async-done(((bf16[1,16,4,16,256]{4,3,2,0,1:T(8,128)(2,1)}), bf16[1,16,4,16,256]{4,3,2,0,1:T(8,128)(2,1)S(1)}, u32[]{:S(2)}, u32[]{:S(2)}) %all-to-all-start.1) | async-done | bytes 524320 | tf_op jit(solution)/shard_map/all_to_all | solution.py:122
  54.9 4.2 %all-to-all-start.3 = ((bf16[1,16,4,16,256]{4,3,2,0,1:T(8,128)(2,1)}), bf16[1,16,4,16,256]{4,3,2,0,1:T(8,128)(2,1)S(1)}, u32[]{:S(2)}, u32[]{:S(2)}) async-start(bf16[1,16,4,16,256]{4,3,2,0,1:T(8,128)(2,1)} %bitcast_bitcast_fusion.2), calls=%async_computation.3 | async-start | bytes 1048576 | tf_op jit(solution)/shard_map/all_to_all | solution.py:129
  59.1 14.2 %all-to-all-done.3 = bf16[1,16,4,16,256]{4,3,2,0,1:T(8,128)(2,1)S(1)} async-done(((bf16[1,16,4,16,256]{4,3,2,0,1:T(8,128)(2,1)}), bf16[1,16,4,16,256]{4,3,2,0,1:T(8,128)(2,1)S(1)}, u32[]{:S(2)}, u32[]{:S(2)}) %all-to-all-start.3) | async-done | bytes 524320 | tf_op jit(solution)/shard_map/all_to_all | solution.py:129
  74.4 28.8 %all_to_all.198 = f32[4,16,16,2,128]{4,2,3,0,1:T(8,128)S(1)} all-to-all(f32[4,16,16,2,128]{4,2,3,0,1:T(8,128)S(1)} %copy.90), channel_id=1, replica_groups=mesh['row'=16,'ch'=2] {'row'}, dimensions={1} | all-to-all | bytes 2097152 | tf_op jit(solution)/shard_map/all_to_all | solution.py:149
  103.2 1.1 copy.91
  104.3 3.6 %all-to-all-start.5 = ((f32[64,1,16,2,128]{4,2,1,0,3:T(8,128)}), f32[64,1,16,2,128]{4,2,1,0,3:T(8,128)S(1)}, u32[]{:S(2)}, u32[]{:S(2)}) async-start(f32[64,1,16,2,128]{4,2,1,0,3:T(8,128)} %copy.91), calls=%async_computation.5 | async-start | bytes 2097152 | tf_op jit(solution)/shard_map/all_to_all | solution.py:148
  108.4 2.0 fusion.11
  110.4 12.4 %all-to-all-done.5 = f32[64,1,16,2,128]{4,2,1,0,3:T(8,128)S(1)} async-done(((f32[64,1,16,2,128]{4,2,1,0,3:T(8,128)}), f32[64,1,16,2,128]{4,2,1,0,3:T(8,128)S(1)}, u32[]{:S(2)}, u32[]{:S(2)}) %all-to-all-start.5) | async-done | bytes 1048608 | tf_op jit(solution)/shard_map/all_to_all | solution.py:148
  126.0 1.2 copy.102
  127.2 3.5 %all-to-all-start.8 = ((bf16[2,16,4,16,128]{4,3,2,1,0:T(8,128)(2,1)}), bf16[2,16,4,16,128]{4,3,2,1,0:T(8,128)(2,1)S(1)}, u32[]{:S(2)}, u32[]{:S(2)}) async-start(bf16[2,16,4,16,128]{4,3,2,1,0:T(8,128)(2,1)} %bitcast.49), calls=%async_computation.8 | async-start | bytes 1048576 | tf_op jit(solution)/shard_map/all_to_all | solution.py:130
  130.7 1.2 copy.98
  131.9 7.3 %all-to-all-done.8 = bf16[2,16,4,16,128]{4,3,2,1,0:T(8,128)(2,1)S(1)} async-done(((bf16[2,16,4,16,128]{4,3,2,1,0:T(8,128)(2,1)}), bf16[2,16,4,16,128]{4,3,2,1,0:T(8,128)(2,1)S(1)}, u32[]{:S(2)}, u32[]{:S(2)}) %all-to-all-start.8) | async-done | bytes 524320 | tf_op jit(solution)/shard_map/all_to_all | solution.py:130
  139.2 3.5 %all-to-all-start.6 = ((bf16[2,16,4,16,128]{4,3,2,1,0:T(8,128)(2,1)}), bf16[2,16,4,16,128]{4,3,2,1,0:T(8,128)(2,1)S(1)}, u32[]{:S(2)}, u32[]{:S(2)}) async-start(bf16[2,16,4,16,128]{4,3,2,1,0:T(8,128)(2,1)} %bitcast.42), calls=%async_computation.6 | async-start | bytes 1048576 | tf_op jit(solution)/shard_map/all_to_all | solution.py:123
  143.6 6.8 %all-to-all-done.6 = bf16[2,16,4,16,128]{4,3,2,1,0:T(8,128)(2,1)S(1)} async-done(((bf16[2,16,4,16,128]{4,3,2,1,0:T(8,128)(2,1)}), bf16[2,16,4,16,128]{4,3,2,1,0:T(8,128)(2,1)S(1)}, u32[]{:S(2)}, u32[]{:S(2)}) %all-to-all-start.6) | async-done | bytes 524320 | tf_op jit(solution)/shard_map/all_to_all | solution.py:123
  150.4 3.6 %all-to-all-start.9 = ((bf16[1,16,4,16,256]{4,3,2,0,1:T(8,128)(2,1)}), bf16[1,16,4,16,256]{4,3,2,0,1:T(8,128)(2,1)S(1)}, u32[]{:S(2)}, u32[]{:S(2)}) async-start(bf16[1,16,4,16,256]{4,3,2,0,1:T(8,128)(2,1)} %bitcast_bitcast_fusion), calls=%async_computation.9 | async-start | bytes 1048576 | tf_op jit(solution)/shard_map/all_to_all | solution.py:129
  154.8 13.4 %all-to-all-done.9 = bf16[1,16,4,16,256]{4,3,2,0,1:T(8,128)(2,1)S(1)} async-done(((bf16[1,16,4,16,256]{4,3,2,0,1:T(8,128)(2,1)}), bf16[1,16,4,16,256]{4,3,2,0,1:T(8,128)(2,1)S(1)}, u32[]{:S(2)}, u32[]{:S(2)}) %all-to-all-start.9) | async-done | bytes 524320 | tf_op jit(solution)/shard_map/all_to_all | solution.py:129
  168.2 4.1 %all-to-all-start.7 = ((bf16[1,16,4,16,256]{4,3,2,0,1:T(8,128)(2,1)}), bf16[1,16,4,16,256]{4,3,2,0,1:T(8,128)(2,1)S(1)}, u32[]{:S(2)}, u32[]{:S(2)}) async-start(bf16[1,16,4,16,256]{4,3,2,0,1:T(8,128)(2,1)} %bitcast_bitcast_fusion.1), calls=%async_computation.7 | async-start | bytes 1048576 | tf_op jit(solution)/shard_map/all_to_all | solution.py:122
  172.3 14.2 %all-to-all-done.7 = bf16[1,16,4,16,256]{4,3,2,0,1:T(8,128)(2,1)S(1)} async-done(((bf16[1,16,4,16,256]{4,3,2,0,1:T(8,128)(2,1)}), bf16[1,16,4,16,256]{4,3,2,0,1:T(8,128)(2,1)S(1)}, u32[]{:S(2)}, u32[]{:S(2)}) %all-to-all-start.7) | async-done | bytes 524320 | tf_op jit(solution)/shard_map/all_to_all | solution.py:122
  187.6 28.6 %all_to_all.199 = f32[4,16,16,2,128]{4,2,3,0,1:T(8,128)S(1)} all-to-all(f32[4,16,16,2,128]{4,2,3,0,1:T(8,128)S(1)} %copy.107), channel_id=1, replica_groups=mesh['row'=16,'ch'=2] {'row'}, dimensions={1} | all-to-all | bytes 2097152 | tf_op jit(solution)/shard_map/all_to_all | solution.py:149
  217.3 3.6 %all-to-all-start.11 = ((f32[64,1,16,2,128]{4,2,1,0,3:T(8,128)}), f32[64,1,16,2,128]{4,2,1,0,3:T(8,128)S(1)}, u32[]{:S(2)}, u32[]{:S(2)}) async-start(f32[64,1,16,2,128]{4,2,1,0,3:T(8,128)} %copy.108), calls=%async_computation.11 | async-start | bytes 2097152 | tf_op jit(solution)/shard_map/all_to_all | solution.py:148
  221.6 14.3 %all-to-all-done.11 = f32[64,1,16,2,128]{4,2,1,0,3:T(8,128)S(1)} async-done(((f32[64,1,16,2,128]{4,2,1,0,3:T(8,128)}), f32[64,1,16,2,128]{4,2,1,0,3:T(8,128)S(1)}, u32[]{:S(2)}, u32[]{:S(2)}) %all-to-all-start.11) | async-done | bytes 1048608 | tf_op jit(solution)/shard_map/all_to_all | solution.py:148
  236.9 1.3 copy.111
  (68 shorter events, 15.8 us)
Async XLA Ops:
  10.6 13.0 %all-to-all-start = ((bf16[2,16,4,16,128]{4,3,2,1,0:T(8,128)(2,1)}), bf16[2,16,4,16,128]{4,3,2,1,0:T(8,128)(2,1)S(1)}, u32[]{:S(2)}, u32[]{:S(2)}) async-start(bf16[2,16,4,16,128]{4,3,2,1,0:T(8,128)(2,1)} %bitcast.9), calls=%async_computation | async-start | bytes 1048576 | tf_op jit(solution)/shard_map/all_to_all | solution.py:123
  23.6 11.2 %all-to-all-start.2 = ((bf16[2,16,4,16,128]{4,3,2,1,0:T(8,128)(2,1)}), bf16[2,16,4,16,128]{4,3,2,1,0:T(8,128)(2,1)S(1)}, u32[]{:S(2)}, u32[]{:S(2)}) async-start(bf16[2,16,4,16,128]{4,3,2,1,0:T(8,128)(2,1)} %bitcast.16), calls=%async_computation.2 | async-start | bytes 1048576 | tf_op jit(solution)/shard_map/all_to_all | solution.py:130
  34.7 20.1 %all-to-all-start.1 = ((bf16[1,16,4,16,256]{4,3,2,0,1:T(8,128)(2,1)}), bf16[1,16,4,16,256]{4,3,2,0,1:T(8,128)(2,1)S(1)}, u32[]{:S(2)}, u32[]{:S(2)}) async-start(bf16[1,16,4,16,256]{4,3,2,0,1:T(8,128)(2,1)} %bitcast_bitcast_fusion.3), calls=%async_computation.1 | async-start | bytes 1048576 | tf_op jit(solution)/shard_map/all_to_all | solution.py:122
  54.9 18.4 %all-to-all-start.3 = ((bf16[1,16,4,16,256]{4,3,2,0,1:T(8,128)(2,1)}), bf16[1,16,4,16,256]{4,3,2,0,1:T(8,128)(2,1)S(1)}, u32[]{:S(2)}, u32[]{:S(2)}) async-start(bf16[1,16,4,16,256]{4,3,2,0,1:T(8,128)(2,1)} %bitcast_bitcast_fusion.2), calls=%async_computation.3 | async-start | bytes 1048576 | tf_op jit(solution)/shard_map/all_to_all | solution.py:129
  74.3 33.6 %copy-start.5 = (f32[2,128]{1,0:T(2,128)S(1)}, f32[2,128]{1,0:T(2,128)}, u32[]{:S(2)}) copy-start(f32[2,128]{1,0:T(2,128)} %param.21) | copy-start | bytes 3076
  74.3 33.6 %copy-start.6 = (f32[2,128]{1,0:T(2,128)S(1)}, f32[2,128]{1,0:T(2,128)}, u32[]{:S(2)}) copy-start(f32[2,128]{1,0:T(2,128)} %param.20) | copy-start | bytes 3076
  74.3 33.6 %copy-start = (f32[16,128,128]{2,1,0:T(8,128)S(1)}, f32[16,128,128]{2,1,0:T(8,128)}, u32[]{:S(2)}) copy-start(f32[16,128,128]{2,1,0:T(8,128)} %param.12) | copy-start | bytes 3145732
  74.4 34.0 %copy-start.4 = (f32[2,128]{1,0:T(2,128)S(1)}, f32[2,128]{1,0:T(2,128)}, u32[]{:S(2)}) copy-start(f32[2,128]{1,0:T(2,128)} %param.23) | copy-start | bytes 3076
  74.4 34.0 %copy-start.7 = (bf16[2,128,128]{2,1,0:T(8,128)(2,1)S(1)}, bf16[2,128,128]{2,1,0:T(8,128)(2,1)}, u32[]{:S(2)}) copy-start(bf16[2,128,128]{2,1,0:T(8,128)(2,1)} %param.18) | copy-start | bytes 196612
  104.3 18.6 %all-to-all-start.5 = ((f32[64,1,16,2,128]{4,2,1,0,3:T(8,128)}), f32[64,1,16,2,128]{4,2,1,0,3:T(8,128)S(1)}, u32[]{:S(2)}, u32[]{:S(2)}) async-start(f32[64,1,16,2,128]{4,2,1,0,3:T(8,128)} %copy.91), calls=%async_computation.5 | async-start | bytes 2097152 | tf_op jit(solution)/shard_map/all_to_all | solution.py:148
  108.4 15.1 %copy-start.3 = (bf16[2,128,128]{2,1,0:T(8,128)(2,1)S(1)}, bf16[2,128,128]{2,1,0:T(8,128)(2,1)}, u32[]{:S(2)}) copy-start(bf16[2,128,128]{2,1,0:T(8,128)(2,1)} %param.22) | copy-start | bytes 196612
  110.4 14.1 %copy-start.2 = (bf16[2,128,512]{2,1,0:T(8,128)(2,1)S(1)}, bf16[2,128,512]{2,1,0:T(8,128)(2,1)}, u32[]{:S(2)}) copy-start(bf16[2,128,512]{2,1,0:T(8,128)(2,1)} %param.16) | copy-start | bytes 786436
  122.8 1.2 copy-start.1
  127.2 12.0 %all-to-all-start.8 = ((bf16[2,16,4,16,128]{4,3,2,1,0:T(8,128)(2,1)}), bf16[2,16,4,16,128]{4,3,2,1,0:T(8,128)(2,1)S(1)}, u32[]{:S(2)}, u32[]{:S(2)}) async-start(bf16[2,16,4,16,128]{4,3,2,1,0:T(8,128)(2,1)} %bitcast.49), calls=%async_computation.8 | async-start | bytes 1048576 | tf_op jit(solution)/shard_map/all_to_all | solution.py:130
  139.2 11.2 %all-to-all-start.6 = ((bf16[2,16,4,16,128]{4,3,2,1,0:T(8,128)(2,1)}), bf16[2,16,4,16,128]{4,3,2,1,0:T(8,128)(2,1)S(1)}, u32[]{:S(2)}, u32[]{:S(2)}) async-start(bf16[2,16,4,16,128]{4,3,2,1,0:T(8,128)(2,1)} %bitcast.42), calls=%async_computation.6 | async-start | bytes 1048576 | tf_op jit(solution)/shard_map/all_to_all | solution.py:123
  150.4 17.8 %all-to-all-start.9 = ((bf16[1,16,4,16,256]{4,3,2,0,1:T(8,128)(2,1)}), bf16[1,16,4,16,256]{4,3,2,0,1:T(8,128)(2,1)S(1)}, u32[]{:S(2)}, u32[]{:S(2)}) async-start(bf16[1,16,4,16,256]{4,3,2,0,1:T(8,128)(2,1)} %bitcast_bitcast_fusion), calls=%async_computation.9 | async-start | bytes 1048576 | tf_op jit(solution)/shard_map/all_to_all | solution.py:129
  168.2 18.4 %all-to-all-start.7 = ((bf16[1,16,4,16,256]{4,3,2,0,1:T(8,128)(2,1)}), bf16[1,16,4,16,256]{4,3,2,0,1:T(8,128)(2,1)S(1)}, u32[]{:S(2)}, u32[]{:S(2)}) async-start(bf16[1,16,4,16,256]{4,3,2,0,1:T(8,128)(2,1)} %bitcast_bitcast_fusion.1), calls=%async_computation.7 | async-start | bytes 1048576 | tf_op jit(solution)/shard_map/all_to_all | solution.py:122
  187.5 33.6 %copy-start.8 = (bf16[2,128,128]{2,1,0:T(8,128)(2,1)S(1)}, bf16[2,128,128]{2,1,0:T(8,128)(2,1)}, u32[]{:S(2)}) copy-start(bf16[2,128,128]{2,1,0:T(8,128)(2,1)} %param.18) | copy-start | bytes 196612
  217.3 18.6 %all-to-all-start.11 = ((f32[64,1,16,2,128]{4,2,1,0,3:T(8,128)}), f32[64,1,16,2,128]{4,2,1,0,3:T(8,128)S(1)}, u32[]{:S(2)}, u32[]{:S(2)}) async-start(f32[64,1,16,2,128]{4,2,1,0,3:T(8,128)} %copy.108), calls=%async_computation.11 | async-start | bytes 2097152 | tf_op jit(solution)/shard_map/all_to_all | solution.py:148
where the time goes:
time: 240 us; the launch traced here: 238 us
  waiting for transfers between devices  110 us (46%)
  blocking collectives  57.4 us (24%)
  starting transfers between devices  39.6 us (16%)
  local copies, waits for them, and re-layouts  16.7 us (7%)
  matrix products  6.89 us (3%)
  other arithmetic  6.83 us (3%)
    all_to_all x2, blocking collectives, local(): lax.all_to_all(returned, 'row', split_axis=1, concat_axis=0, tiled=True)  57.4 us
    all_to_all x2, waiting for transfers between devices, local(): lax.all_to_all(lax.all_to_all(send_left, 'ch', split_axis=0, concat_axis=...  27.6 us
    all_to_all x2, waiting for transfers between devices, local(): lax.all_to_all(lax.all_to_all(send_right, 'ch', split_axis=0, concat_axis...  27.6 us
    all_to_all x2, waiting for transfers between devices, local(): lax.all_to_all(lax.all_to_all(returned, 'row', split_axis=1, concat_axis=...  26.7 us
    all_to_all x2, waiting for transfers between devices, local(): lax.all_to_all(send_left, 'ch', split_axis=0, concat_axis=4, tiled=True)  14.4 us
    all_to_all x2, waiting for transfers between devices, local(): lax.all_to_all(send_right, 'ch', split_axis=0, concat_axis=4, tiled=True)  14.1 us
    all_to_all x2, starting transfers between devices, local(): lax.all_to_all(lax.all_to_all(send_left, 'ch', split_axis=0, concat_axis=...  9.96 us
    all_to_all x2, starting transfers between devices, local(): lax.all_to_all(send_left, 'ch', split_axis=0, concat_axis=4, tiled=True)  7.75 us
  transfers between devices with their start and end apart: 10, of which 10 were waited for; matrix products, arithmetic and copies ran while one was open for 4% of the time, Pallas kernels for 0%

commit v1 on v0

--- a/solution.py
+++ b/solution.py
@@ -1,3 +1,4 @@
+import functools
 import jax
 import jax.numpy as jnp
 from jax import lax
@@ -5,6 +6,38 @@
 
 PAIR_EPSILON = 1e-05
 HIDDEN_EPSILON = 1.0
+
+
+def floor_point(inp, axis_no, chunk):
+    a_now, x_new = (inp.shape[:axis_no], inp.shape[axis_no + 1 :])
+    heard = jnp.moveaxis(inp.reshape(*a_now, chunk, -1, *x_new), axis_no, 0)
+    return heard
+
+
+def produce_spots(in_array, dimension_no):
+    v1 = list(in_array.shape[1:])
+    v1[dimension_no] *= in_array.shape[0]
+    v_now = jnp.moveaxis(in_array, 0, dimension_no).reshape(v1)
+    return v_now
+
+
+def draw_clusters(z_in, lane_axis, xx, inner_x):
+    field_out, finding = (jax.lax.psum(1, axis_name=lane_axis), jax.lax.axis_index(lane_axis))
+    t1 = floor_point(z_in, xx, field_out)
+    trail = [t1[finding]]
+    for dd in [*range(1, field_out)]:
+        big = t1[finding ^ dd]
+        trail.append(
+            jax.lax.ppermute(
+                big, axis_name=lane_axis, perm=[(k0, k0 ^ dd) for k0 in range(field_out)]
+            )
+        )
+    t1 = jnp.stack(trail, axis=0)[finding ^ jnp.arange(field_out)]
+    w2 = produce_spots(t1, inner_x)
+    return w2
+
+
+define_loops = functools.partial(draw_clusters, lane_axis="row", xx=1, inner_x=0)
 
 
 def layer_norm(values, gain_value, shift_value, along, epsilon):
@@ -146,11 +179,7 @@
             )
         returned = products.reshape(per_slot, row_total, sub_rows, col_total, col_count)
         gathered = lax.all_to_all(
-            lax.all_to_all(returned, "row", split_axis=1, concat_axis=0, tiled=True),
-            "ch",
-            split_axis=3,
-            concat_axis=0,
-            tiled=True,
+            define_loops(returned), "ch", split_axis=3, concat_axis=0, tiled=True
         )
         gathered = gathered.reshape(col_total, slots, quarters, per_slot, sub_rows, col_count)
         gathered = jnp.transpose(gathered, (0, 1, 3, 2, 4, 5)).reshape(

time: 240 us -> 247 us (1.029)
  blocking collectives: 57.4 us -> 0 us
  starting transfers between devices: 39.6 us -> 83.3 us
  waiting for transfers between devices: 110 us -> 125 us
  local copies, waits for them, and re-layouts: 16.7 us -> 20.2 us
    all_to_all x2 -> x0, blocking collectives: 57.4 us -> none  [local(): lax.all_to_all(returned, 'row', split_axis=1, concat_axis=0, tiled=True)]
    ppermute x0 -> x30, starting transfers between devices: none -> 41.8 us  [draw_clusters(): jax.lax.ppermute(big, axis_name=lane_axis, perm=[(k0, k0 ^ dd) for k0 in...]
    ppermute x0 -> x30, waiting for transfers between devices: none -> 19.9 us  [draw_clusters(): jax.lax.ppermute(big, axis_name=lane_axis, perm=[(k0, k0 ^ dd) for k0 in...]
  transfers between devices with their start and end apart: 10 -> 40, of which waited for: 10 -> 18; matrix products, arithmetic and copies ran while one was open for 4% -> 5% of each run, Pallas kernels for 0% -> 0%
where the time goes in v1:
time: 247 us; the launch traced here: 245 us
  waiting for transfers between devices  125 us (51%)
  starting transfers between devices  83.3 us (34%)
  local copies, waits for them, and re-layouts  20.2 us (8%)
  matrix products  8.69 us (4%)
  other arithmetic  6.84 us (3%)
    ppermute x30, starting transfers between devices, draw_clusters(): jax.lax.ppermute(big, axis_name=lane_axis, perm=[(k0, k0 ^ dd) for k0 in...  41.8 us
    all_to_all x2, waiting for transfers between devices, local(): lax.all_to_all(lax.all_to_all(send_right, 'ch', split_axis=0, concat_axis...  27.5 us
    all_to_all x2, waiting for transfers between devices, local(): lax.all_to_all(lax.all_to_all(send_left, 'ch', split_axis=0, concat_axis=...  26.8 us
    all_to_all x2, waiting for transfers between devices, local(): lax.all_to_all(define_loops(returned), 'ch', split_axis=3, concat_axis=0,...  24.3 us
    ppermute x30, waiting for transfers between devices, draw_clusters(): jax.lax.ppermute(big, axis_name=lane_axis, perm=[(k0, k0 ^ dd) for k0 in...  19.9 us
    all_to_all x2, waiting for transfers between devices, local(): lax.all_to_all(send_left, 'ch', split_axis=0, concat_axis=4, tiled=True)  13.5 us
    all_to_all x2, waiting for transfers between devices, local(): lax.all_to_all(send_right, 'ch', split_axis=0, concat_axis=4, tiled=True)  13.4 us
    all_to_all x2, starting transfers between devices, local(): lax.all_to_all(lax.all_to_all(send_left, 'ch', split_axis=0, concat_axis=...  10 us
  transfers between devices with their start and end apart: 40, of which 18 were waited for; matrix products, arithmetic and copies ran while one was open for 5% of the time, Pallas kernels for 0%

profile of v1, /device:TPU:0, one launch (start us, length us, event | category | flops | bytes accessed | tf_op | source)
XLA Modules:
  0.0 245.2 jit_solution(12804214279707997324)
XLA Ops:
  6.7 2.1 add_bitcast_fusion.1
  10.6 4.3 %all-to-all-start = ((bf16[2,16,4,16,128]{4,3,2,1,0:T(8,128)(2,1)}), bf16[2,16,4,16,128]{4,3,2,1,0:T(8,128)(2,1)S(1)}, u32[]{:S(2)}, u32[]{:S(2)}) async-start(bf16[2,16,4,16,128]{4,3,2,1,0:T(8,128)(2,1)} %bitcast.9), calls=%async_computation | async-start | bytes 1048576 | tf_op jit(solution)/shard_map/all_to_all | solution.py:156
  16.1 7.5 %all-to-all-done = bf16[2,16,4,16,128]{4,3,2,1,0:T(8,128)(2,1)S(1)} async-done(((bf16[2,16,4,16,128]{4,3,2,1,0:T(8,128)(2,1)}), bf16[2,16,4,16,128]{4,3,2,1,0:T(8,128)(2,1)S(1)}, u32[]{:S(2)}, u32[]{:S(2)}) %all-to-all-start) | async-done | bytes 524320 | tf_op jit(solution)/shard_map/all_to_all | solution.py:156
  23.6 3.5 %all-to-all-start.2 = ((bf16[2,16,4,16,128]{4,3,2,1,0:T(8,128)(2,1)}), bf16[2,16,4,16,128]{4,3,2,1,0:T(8,128)(2,1)S(1)}, u32[]{:S(2)}, u32[]{:S(2)}) async-start(bf16[2,16,4,16,128]{4,3,2,1,0:T(8,128)(2,1)} %bitcast.16), calls=%async_computation.2 | async-start | bytes 1048576 | tf_op jit(solution)/shard_map/all_to_all | solution.py:163
  28.0 6.8 %all-to-all-done.2 = bf16[2,16,4,16,128]{4,3,2,1,0:T(8,128)(2,1)S(1)} async-done(((bf16[2,16,4,16,128]{4,3,2,1,0:T(8,128)(2,1)}), bf16[2,16,4,16,128]{4,3,2,1,0:T(8,128)(2,1)S(1)}, u32[]{:S(2)}, u32[]{:S(2)}) %all-to-all-start.2) | async-done | bytes 524320 | tf_op jit(solution)/shard_map/all_to_all | solution.py:163
  34.8 5.8 %all-to-all-start.1 = ((bf16[1,16,4,16,256]{4,3,2,0,1:T(8,128)(2,1)}), bf16[1,16,4,16,256]{4,3,2,0,1:T(8,128)(2,1)S(1)}, u32[]{:S(2)}, u32[]{:S(2)}) async-start(bf16[1,16,4,16,256]{4,3,2,0,1:T(8,128)(2,1)} %bitcast_bitcast_fusion.3), calls=%async_computation.1 | async-start | bytes 1048576 | tf_op jit(solution)/shard_map/all_to_all | solution.py:155
  41.5 13.4 %all-to-all-done.1 = bf16[1,16,4,16,256]{4,3,2,0,1:T(8,128)(2,1)S(1)} async-done(((bf16[1,16,4,16,256]{4,3,2,0,1:T(8,128)(2,1)}), bf16[1,16,4,16,256]{4,3,2,0,1:T(8,128)(2,1)S(1)}, u32[]{:S(2)}, u32[]{:S(2)}) %all-to-all-start.1) | async-done | bytes 524320 | tf_op jit(solution)/shard_map/all_to_all | solution.py:155
  54.9 4.2 %all-to-all-start.3 = ((bf16[1,16,4,16,256]{4,3,2,0,1:T(8,128)(2,1)}), bf16[1,16,4,16,256]{4,3,2,0,1:T(8,128)(2,1)S(1)}, u32[]{:S(2)}, u32[]{:S(2)}) async-start(bf16[1,16,4,16,256]{4,3,2,0,1:T(8,128)(2,1)} %bitcast_bitcast_fusion.2), calls=%async_computation.3 | async-start | bytes 1048576 | tf_op jit(solution)/shard_map/all_to_all | solution.py:162
  59.2 14.1 %all-to-all-done.3 = bf16[1,16,4,16,256]{4,3,2,0,1:T(8,128)(2,1)S(1)} async-done(((bf16[1,16,4,16,256]{4,3,2,0,1:T(8,128)(2,1)}), bf16[1,16,4,16,256]{4,3,2,0,1:T(8,128)(2,1)S(1)}, u32[]{:S(2)}, u32[]{:S(2)}) %all-to-all-start.3) | async-done | bytes 524320 | tf_op jit(solution)/shard_map/all_to_all | solution.py:162
  78.9 2.1 collective-permute-start.5
  81.6 2.5 %collective-permute-start.7 = (f32[4,1,16,2,128]{4,2,3,0,1:T(8,128)S(1)}, f32[4,1,16,2,128]{4,2,3,0,1:T(8,128)S(1)}, u32[]{:S(2)}, u32[]{:S(2)}) collective-permute-start(f32[4,1,16,2,128]{4,2,3,0,1:T(8,128)S(1)} %bitcast.322), channel_id=1, source_target_pairs={{0,16},{2,18},{4,20},{6,22},{8,24},{10,26},{12,28},{14,30},{16,0},... | collective-permute-start | bytes 196616 | tf_op jit(solution)/shard_map/ppermute | solution.py:31
  91.9 4.5 %collective-permute-done.8 = f32[4,1,16,2,128]{4,2,3,0,1:T(8,128)S(1)} collective-permute-done((f32[4,1,16,2,128]{4,2,3,0,1:T(8,128)S(1)}, f32[4,1,16,2,128]{4,2,3,0,1:T(8,128)S(1)}, u32[]{:S(2)}, u32[]{:S(2)}) %collective-permute-start.8) | collective-permute-done | bytes 65568 | tf_op jit(solution)/shard_map/ppermute | solution.py:31
  96.4 2.5 %collective-permute-start.13 = (f32[4,1,16,2,128]{4,2,3,0,1:T(8,128)S(1)}, f32[4,1,16,2,128]{4,2,3,0,1:T(8,128)S(1)}, u32[]{:S(2)}, u32[]{:S(2)}) collective-permute-start(f32[4,1,16,2,128]{4,2,3,0,1:T(8,128)S(1)} %bitcast.310), channel_id=1, source_target_pairs={{0,28},{2,30},{4,24},{6,26},{8,20},{10,22},{12,16},{14,18},{16,12}... | collective-permute-start | bytes 196616 | tf_op jit(solution)/shard_map/ppermute | solution.py:31
  101.1 2.3 collective-permute-done.13
  103.3 2.6 %collective-permute-done.14 = f32[4,1,16,2,128]{4,2,3,0,1:T(8,128)S(1)} collective-permute-done((f32[4,1,16,2,128]{4,2,3,0,1:T(8,128)S(1)}, f32[4,1,16,2,128]{4,2,3,0,1:T(8,128)S(1)}, u32[]{:S(2)}, u32[]{:S(2)}) %collective-permute-start.14) | collective-permute-done | bytes 65568 | tf_op jit(solution)/shard_map/ppermute | solution.py:31
  107.6 3.6 %all-to-all-start.4 = ((f32[64,1,16,2,128]{4,2,0,1,3:T(8,128)}), f32[64,1,16,2,128]{4,2,0,1,3:T(8,128)S(1)}, u32[]{:S(2)}, u32[]{:S(2)}) async-start(f32[64,1,16,2,128]{4,2,0,1,3:T(8,128)} %copy.106), calls=%async_computation.4 | async-start | bytes 2097152 | tf_op jit(solution)/shard_map/all_to_all | solution.py:181
  113.8 11.6 %all-to-all-done.4 = f32[64,1,16,2,128]{4,2,0,1,3:T(8,128)S(1)} async-done(((f32[64,1,16,2,128]{4,2,0,1,3:T(8,128)}), f32[64,1,16,2,128]{4,2,0,1,3:T(8,128)S(1)}, u32[]{:S(2)}, u32[]{:S(2)}) %all-to-all-start.4) | async-done | bytes 1048608 | tf_op jit(solution)/shard_map/all_to_all | solution.py:181
  129.9 3.5 %all-to-all-start.7 = ((bf16[2,16,4,16,128]{4,3,2,1,0:T(8,128)(2,1)}), bf16[2,16,4,16,128]{4,3,2,1,0:T(8,128)(2,1)S(1)}, u32[]{:S(2)}, u32[]{:S(2)}) async-start(bf16[2,16,4,16,128]{4,3,2,1,0:T(8,128)(2,1)} %bitcast.80), calls=%async_computation.7 | async-start | bytes 1048576 | tf_op jit(solution)/shard_map/all_to_all | solution.py:163
  134.6 6.6 %all-to-all-done.7 = bf16[2,16,4,16,128]{4,3,2,1,0:T(8,128)(2,1)S(1)} async-done(((bf16[2,16,4,16,128]{4,3,2,1,0:T(8,128)(2,1)}), bf16[2,16,4,16,128]{4,3,2,1,0:T(8,128)(2,1)S(1)}, u32[]{:S(2)}, u32[]{:S(2)}) %all-to-all-start.7) | async-done | bytes 524320 | tf_op jit(solution)/shard_map/all_to_all | solution.py:163
  141.1 3.5 %all-to-all-start.5 = ((bf16[2,16,4,16,128]{4,3,2,1,0:T(8,128)(2,1)}), bf16[2,16,4,16,128]{4,3,2,1,0:T(8,128)(2,1)S(1)}, u32[]{:S(2)}, u32[]{:S(2)}) async-start(bf16[2,16,4,16,128]{4,3,2,1,0:T(8,128)(2,1)} %bitcast.73), calls=%async_computation.5 | async-start | bytes 1048576 | tf_op jit(solution)/shard_map/all_to_all | solution.py:156
  145.5 6.0 %all-to-all-done.5 = bf16[2,16,4,16,128]{4,3,2,1,0:T(8,128)(2,1)S(1)} async-done(((bf16[2,16,4,16,128]{4,3,2,1,0:T(8,128)(2,1)}), bf16[2,16,4,16,128]{4,3,2,1,0:T(8,128)(2,1)S(1)}, u32[]{:S(2)}, u32[]{:S(2)}) %all-to-all-start.5) | async-done | bytes 524320 | tf_op jit(solution)/shard_map/all_to_all | solution.py:156
  151.5 5.4 %all-to-all-start.8 = ((bf16[1,16,4,16,256]{4,3,2,0,1:T(8,128)(2,1)}), bf16[1,16,4,16,256]{4,3,2,0,1:T(8,128)(2,1)S(1)}, u32[]{:S(2)}, u32[]{:S(2)}) async-start(bf16[1,16,4,16,256]{4,3,2,0,1:T(8,128)(2,1)} %bitcast_bitcast_fusion), calls=%async_computation.8 | async-start | bytes 1048576 | tf_op jit(solution)/shard_map/all_to_all | solution.py:162
  157.8 13.4 %all-to-all-done.8 = bf16[1,16,4,16,256]{4,3,2,0,1:T(8,128)(2,1)S(1)} async-done(((bf16[1,16,4,16,256]{4,3,2,0,1:T(8,128)(2,1)}), bf16[1,16,4,16,256]{4,3,2,0,1:T(8,128)(2,1)S(1)}, u32[]{:S(2)}, u32[]{:S(2)}) %all-to-all-start.8) | async-done | bytes 524320 | tf_op jit(solution)/shard_map/all_to_all | solution.py:162
  171.2 4.2 %all-to-all-start.6 = ((bf16[1,16,4,16,256]{4,3,2,0,1:T(8,128)(2,1)}), bf16[1,16,4,16,256]{4,3,2,0,1:T(8,128)(2,1)S(1)}, u32[]{:S(2)}, u32[]{:S(2)}) async-start(bf16[1,16,4,16,256]{4,3,2,0,1:T(8,128)(2,1)} %bitcast_bitcast_fusion.1), calls=%async_computation.6 | async-start | bytes 1048576 | tf_op jit(solution)/shard_map/all_to_all | solution.py:155
  176.2 13.4 %all-to-all-done.6 = bf16[1,16,4,16,256]{4,3,2,0,1:T(8,128)(2,1)S(1)} async-done(((bf16[1,16,4,16,256]{4,3,2,0,1:T(8,128)(2,1)}), bf16[1,16,4,16,256]{4,3,2,0,1:T(8,128)(2,1)S(1)}, u32[]{:S(2)}, u32[]{:S(2)}) %all-to-all-start.6) | async-done | bytes 524320 | tf_op jit(solution)/shard_map/all_to_all | solution.py:155
  198.9 2.5 %collective-permute-start.22 = (f32[4,1,16,2,128]{4,2,3,0,1:T(8,128)S(1)}, f32[4,1,16,2,128]{4,2,3,0,1:T(8,128)S(1)}, u32[]{:S(2)}, u32[]{:S(2)}) collective-permute-start(f32[4,1,16,2,128]{4,2,3,0,1:T(8,128)S(1)} %bitcast.323), channel_id=1, source_target_pairs={{0,16},{2,18},{4,20},{6,22},{8,24},{10,26},{12,28},{14,30},{16,0},... | collective-permute-start | bytes 196616 | tf_op jit(solution)/shard_map/ppermute | solution.py:31
  209.2 5.2 %collective-permute-done.23 = f32[4,1,16,2,128]{4,2,3,0,1:T(8,128)S(1)} collective-permute-done((f32[4,1,16,2,128]{4,2,3,0,1:T(8,128)S(1)}, f32[4,1,16,2,128]{4,2,3,0,1:T(8,128)S(1)}, u32[]{:S(2)}, u32[]{:S(2)}) %collective-permute-start.23) | collective-permute-done | bytes 65568 | tf_op jit(solution)/shard_map/ppermute | solution.py:31
  216.5 2.2 collective-permute-start.29
  218.8 2.6 %collective-permute-done.28 = f32[4,1,16,2,128]{4,2,3,0,1:T(8,128)S(1)} collective-permute-done((f32[4,1,16,2,128]{4,2,3,0,1:T(8,128)S(1)}, f32[4,1,16,2,128]{4,2,3,0,1:T(8,128)S(1)}, u32[]{:S(2)}, u32[]{:S(2)}) %collective-permute-start.28) | collective-permute-done | bytes 65568 | tf_op jit(solution)/shard_map/ppermute | solution.py:31
  221.4 2.1 collective-permute-done.29
  225.2 3.6 %all-to-all-start.9 = ((f32[64,1,16,2,128]{4,2,1,0,3:T(8,128)}), f32[64,1,16,2,128]{4,2,1,0,3:T(8,128)S(1)}, u32[]{:S(2)}, u32[]{:S(2)}) async-start(f32[64,1,16,2,128]{4,2,1,0,3:T(8,128)} %copy.138), calls=%async_computation.9 | async-start | bytes 2097152 | tf_op jit(solution)/shard_map/all_to_all | solution.py:181
  230.3 12.6 %all-to-all-done.9 = f32[64,1,16,2,128]{4,2,1,0,3:T(8,128)S(1)} async-done(((f32[64,1,16,2,128]{4,2,1,0,3:T(8,128)}), f32[64,1,16,2,128]{4,2,1,0,3:T(8,128)S(1)}, u32[]{:S(2)}, u32[]{:S(2)}) %all-to-all-start.9) | async-done | bytes 1048608 | tf_op jit(solution)/shard_map/all_to_all | solution.py:181
  (190 shorter events, 64.3 us)
Async XLA Ops:
  10.6 13.0 %all-to-all-start = ((bf16[2,16,4,16,128]{4,3,2,1,0:T(8,128)(2,1)}), bf16[2,16,4,16,128]{4,3,2,1,0:T(8,128)(2,1)S(1)}, u32[]{:S(2)}, u32[]{:S(2)}) async-start(bf16[2,16,4,16,128]{4,3,2,1,0:T(8,128)(2,1)} %bitcast.9), calls=%async_computation | async-start | bytes 1048576 | tf_op jit(solution)/shard_map/all_to_all | solution.py:156
  23.6 11.2 %all-to-all-start.2 = ((bf16[2,16,4,16,128]{4,3,2,1,0:T(8,128)(2,1)}), bf16[2,16,4,16,128]{4,3,2,1,0:T(8,128)(2,1)S(1)}, u32[]{:S(2)}, u32[]{:S(2)}) async-start(bf16[2,16,4,16,128]{4,3,2,1,0:T(8,128)(2,1)} %bitcast.16), calls=%async_computation.2 | async-start | bytes 1048576 | tf_op jit(solution)/shard_map/all_to_all | solution.py:163
  34.8 20.1 %all-to-all-start.1 = ((bf16[1,16,4,16,256]{4,3,2,0,1:T(8,128)(2,1)}), bf16[1,16,4,16,256]{4,3,2,0,1:T(8,128)(2,1)S(1)}, u32[]{:S(2)}, u32[]{:S(2)}) async-start(bf16[1,16,4,16,256]{4,3,2,0,1:T(8,128)(2,1)} %bitcast_bitcast_fusion.3), calls=%async_computation.1 | async-start | bytes 1048576 | tf_op jit(solution)/shard_map/all_to_all | solution.py:155
  54.9 18.4 %all-to-all-start.3 = ((bf16[1,16,4,16,256]{4,3,2,0,1:T(8,128)(2,1)}), bf16[1,16,4,16,256]{4,3,2,0,1:T(8,128)(2,1)S(1)}, u32[]{:S(2)}, u32[]{:S(2)}) async-start(bf16[1,16,4,16,256]{4,3,2,0,1:T(8,128)(2,1)} %bitcast_bitcast_fusion.2), calls=%async_computation.3 | async-start | bytes 1048576 | tf_op jit(solution)/shard_map/all_to_all | solution.py:162
  76.9 7.2 %collective-permute-start.3 = (f32[4,1,16,2,128]{4,2,3,0,1:T(8,128)S(1)}, f32[4,1,16,2,128]{4,2,3,0,1:T(8,128)S(1)}, u32[]{:S(2)}, u32[]{:S(2)}) collective-permute-start(f32[4,1,16,2,128]{4,2,3,0,1:T(8,128)S(1)} %bitcast.330), channel_id=1, source_target_pairs={{0,8},{2,10},{4,12},{6,14},{8,0},{10,2},{12,4},{14,6},{16,24},{18,... | collective-permute-start | bytes 196616 | tf_op jit(solution)/shard_map/ppermute | solution.py:31
  78.9 7.5 %collective-permute-start.5 = (f32[4,1,16,2,128]{4,2,3,0,1:T(8,128)S(1)}, f32[4,1,16,2,128]{4,2,3,0,1:T(8,128)S(1)}, u32[]{:S(2)}, u32[]{:S(2)}) collective-permute-start(f32[4,1,16,2,128]{4,2,3,0,1:T(8,128)S(1)} %bitcast.326), channel_id=1, source_target_pairs={{0,12},{2,14},{4,8},{6,10},{8,4},{10,6},{12,0},{14,2},{16,28},{18,... | collective-permute-start | bytes 196616 | tf_op jit(solution)/shard_map/ppermute | solution.py:31
  81.0 7.1 %collective-permute-start.6 = (f32[4,1,16,2,128]{4,2,3,0,1:T(8,128)S(1)}, f32[4,1,16,2,128]{4,2,3,0,1:T(8,128)S(1)}, u32[]{:S(2)}, u32[]{:S(2)}) collective-permute-start(f32[4,1,16,2,128]{4,2,3,0,1:T(8,128)S(1)} %bitcast.324), channel_id=1, source_target_pairs={{0,14},{2,12},{4,10},{6,8},{8,6},{10,4},{12,2},{14,0},{16,30},{18,... | collective-permute-start | bytes 196616 | tf_op jit(solution)/shard_map/ppermute | solution.py:31
  81.6 8.5 %collective-permute-start.7 = (f32[4,1,16,2,128]{4,2,3,0,1:T(8,128)S(1)}, f32[4,1,16,2,128]{4,2,3,0,1:T(8,128)S(1)}, u32[]{:S(2)}, u32[]{:S(2)}) collective-permute-start(f32[4,1,16,2,128]{4,2,3,0,1:T(8,128)S(1)} %bitcast.322), channel_id=1, source_target_pairs={{0,16},{2,18},{4,20},{6,22},{8,24},{10,26},{12,28},{14,30},{16,0},... | collective-permute-start | bytes 196616 | tf_op jit(solution)/shard_map/ppermute | solution.py:31
  84.1 12.3 %collective-permute-start.8 = (f32[4,1,16,2,128]{4,2,3,0,1:T(8,128)S(1)}, f32[4,1,16,2,128]{4,2,3,0,1:T(8,128)S(1)}, u32[]{:S(2)}, u32[]{:S(2)}) collective-permute-start(f32[4,1,16,2,128]{4,2,3,0,1:T(8,128)S(1)} %bitcast.320), channel_id=1, source_target_pairs={{0,18},{2,16},{4,22},{6,20},{8,26},{10,24},{12,30},{14,28},{16,2},... | collective-permute-start | bytes 196616 | tf_op jit(solution)/shard_map/ppermute | solution.py:31
  84.5 14.6 %collective-permute-start.9 = (f32[4,1,16,2,128]{4,2,3,0,1:T(8,128)S(1)}, f32[4,1,16,2,128]{4,2,3,0,1:T(8,128)S(1)}, u32[]{:S(2)}, u32[]{:S(2)}) collective-permute-start(f32[4,1,16,2,128]{4,2,3,0,1:T(8,128)S(1)} %bitcast.318), channel_id=1, source_target_pairs={{0,20},{2,22},{4,16},{6,18},{8,28},{10,30},{12,24},{14,26},{16,4},... | collective-permute-start | bytes 196616 | tf_op jit(solution)/shard_map/ppermute | solution.py:31
  86.4 14.6 %collective-permute-start.10 = (f32[4,1,16,2,128]{4,2,3,0,1:T(8,128)S(1)}, f32[4,1,16,2,128]{4,2,3,0,1:T(8,128)S(1)}, u32[]{:S(2)}, u32[]{:S(2)}) collective-permute-start(f32[4,1,16,2,128]{4,2,3,0,1:T(8,128)S(1)} %bitcast.316), channel_id=1, source_target_pairs={{0,22},{2,20},{4,18},{6,16},{8,30},{10,28},{12,26},{14,24},{16,6},... | collective-permute-start | bytes 196616 | tf_op jit(solution)/shard_map/ppermute | solution.py:31
  88.1 12.9 %collective-permute-start.11 = (f32[4,1,16,2,128]{4,2,3,0,1:T(8,128)S(1)}, f32[4,1,16,2,128]{4,2,3,0,1:T(8,128)S(1)}, u32[]{:S(2)}, u32[]{:S(2)}) collective-permute-start(f32[4,1,16,2,128]{4,2,3,0,1:T(8,128)S(1)} %bitcast.314), channel_id=1, source_target_pairs={{0,24},{2,26},{4,28},{6,30},{8,16},{10,18},{12,20},{14,22},{16,8},... | collective-permute-start | bytes 196616 | tf_op jit(solution)/shard_map/ppermute | solution.py:31
  90.1 10.9 %collective-permute-start.12 = (f32[4,1,16,2,128]{4,2,3,0,1:T(8,128)S(1)}, f32[4,1,16,2,128]{4,2,3,0,1:T(8,128)S(1)}, u32[]{:S(2)}, u32[]{:S(2)}) collective-permute-start(f32[4,1,16,2,128]{4,2,3,0,1:T(8,128)S(1)} %bitcast.312), channel_id=1, source_target_pairs={{0,26},{2,24},{4,30},{6,28},{8,18},{10,16},{12,22},{14,20},{16,10}... | collective-permute-start | bytes 196616 | tf_op jit(solution)/shard_map/ppermute | solution.py:31
  96.4 7.0 %collective-permute-start.13 = (f32[4,1,16,2,128]{4,2,3,0,1:T(8,128)S(1)}, f32[4,1,16,2,128]{4,2,3,0,1:T(8,128)S(1)}, u32[]{:S(2)}, u32[]{:S(2)}) collective-permute-start(f32[4,1,16,2,128]{4,2,3,0,1:T(8,128)S(1)} %bitcast.310), channel_id=1, source_target_pairs={{0,28},{2,30},{4,24},{6,26},{8,20},{10,22},{12,16},{14,18},{16,12}... | collective-permute-start | bytes 196616 | tf_op jit(solution)/shard_map/ppermute | solution.py:31
  99.1 6.8 %collective-permute-start.14 = (f32[4,1,16,2,128]{4,2,3,0,1:T(8,128)S(1)}, f32[4,1,16,2,128]{4,2,3,0,1:T(8,128)S(1)}, u32[]{:S(2)}, u32[]{:S(2)}) collective-permute-start(f32[4,1,16,2,128]{4,2,3,0,1:T(8,128)S(1)} %bitcast.308), channel_id=1, source_target_pairs={{0,30},{2,28},{4,26},{6,24},{8,22},{10,20},{12,18},{14,16},{16,14}... | collective-permute-start | bytes 196616 | tf_op jit(solution)/shard_map/ppermute | solution.py:31
  107.6 17.8 %all-to-all-start.4 = ((f32[64,1,16,2,128]{4,2,0,1,3:T(8,128)}), f32[64,1,16,2,128]{4,2,0,1,3:T(8,128)S(1)}, u32[]{:S(2)}, u32[]{:S(2)}) async-start(f32[64,1,16,2,128]{4,2,0,1,3:T(8,128)} %copy.106), calls=%async_computation.4 | async-start | bytes 2097152 | tf_op jit(solution)/shard_map/all_to_all | solution.py:181
  129.9 11.3 %all-to-all-start.7 = ((bf16[2,16,4,16,128]{4,3,2,1,0:T(8,128)(2,1)}), bf16[2,16,4,16,128]{4,3,2,1,0:T(8,128)(2,1)S(1)}, u32[]{:S(2)}, u32[]{:S(2)}) async-start(bf16[2,16,4,16,128]{4,3,2,1,0:T(8,128)(2,1)} %bitcast.80), calls=%async_computation.7 | async-start | bytes 1048576 | tf_op jit(solution)/shard_map/all_to_all | solution.py:163
  141.1 10.4 %all-to-all-start.5 = ((bf16[2,16,4,16,128]{4,3,2,1,0:T(8,128)(2,1)}), bf16[2,16,4,16,128]{4,3,2,1,0:T(8,128)(2,1)S(1)}, u32[]{:S(2)}, u32[]{:S(2)}) async-start(bf16[2,16,4,16,128]{4,3,2,1,0:T(8,128)(2,1)} %bitcast.73), calls=%async_computation.5 | async-start | bytes 1048576 | tf_op jit(solution)/shard_map/all_to_all | solution.py:156
  151.5 19.7 %all-to-all-start.8 = ((bf16[1,16,4,16,256]{4,3,2,0,1:T(8,128)(2,1)}), bf16[1,16,4,16,256]{4,3,2,0,1:T(8,128)(2,1)S(1)}, u32[]{:S(2)}, u32[]{:S(2)}) async-start(bf16[1,16,4,16,256]{4,3,2,0,1:T(8,128)(2,1)} %bitcast_bitcast_fusion), calls=%async_computation.8 | async-start | bytes 1048576 | tf_op jit(solution)/shard_map/all_to_all | solution.py:162
  171.2 18.4 %all-to-all-start.6 = ((bf16[1,16,4,16,256]{4,3,2,0,1:T(8,128)(2,1)}), bf16[1,16,4,16,256]{4,3,2,0,1:T(8,128)(2,1)S(1)}, u32[]{:S(2)}, u32[]{:S(2)}) async-start(bf16[1,16,4,16,256]{4,3,2,0,1:T(8,128)(2,1)} %bitcast_bitcast_fusion.1), calls=%async_computation.6 | async-start | bytes 1048576 | tf_op jit(solution)/shard_map/all_to_all | solution.py:155
  194.2 7.2 %collective-permute-start.18 = (f32[4,1,16,2,128]{4,2,3,0,1:T(8,128)S(1)}, f32[4,1,16,2,128]{4,2,3,0,1:T(8,128)S(1)}, u32[]{:S(2)}, u32[]{:S(2)}) collective-permute-start(f32[4,1,16,2,128]{4,2,3,0,1:T(8,128)S(1)} %bitcast.331), channel_id=1, source_target_pairs={{0,8},{2,10},{4,12},{6,14},{8,0},{10,2},{12,4},{14,6},{16,24},{18,... | collective-permute-start | bytes 196616 | tf_op jit(solution)/shard_map/ppermute | solution.py:31
  196.2 7.5 %collective-permute-start.20 = (f32[4,1,16,2,128]{4,2,3,0,1:T(8,128)S(1)}, f32[4,1,16,2,128]{4,2,3,0,1:T(8,128)S(1)}, u32[]{:S(2)}, u32[]{:S(2)}) collective-permute-start(f32[4,1,16,2,128]{4,2,3,0,1:T(8,128)S(1)} %bitcast.327), channel_id=1, source_target_pairs={{0,12},{2,14},{4,8},{6,10},{8,4},{10,6},{12,0},{14,2},{16,28},{18,... | collective-permute-start | bytes 196616 | tf_op jit(solution)/shard_map/ppermute | solution.py:31
  198.3 7.1 %collective-permute-start.21 = (f32[4,1,16,2,128]{4,2,3,0,1:T(8,128)S(1)}, f32[4,1,16,2,128]{4,2,3,0,1:T(8,128)S(1)}, u32[]{:S(2)}, u32[]{:S(2)}) collective-permute-start(f32[4,1,16,2,128]{4,2,3,0,1:T(8,128)S(1)} %bitcast.325), channel_id=1, source_target_pairs={{0,14},{2,12},{4,10},{6,8},{8,6},{10,4},{12,2},{14,0},{16,30},{18,... | collective-permute-start | bytes 196616 | tf_op jit(solution)/shard_map/ppermute | solution.py:31
  198.9 8.5 %collective-permute-start.22 = (f32[4,1,16,2,128]{4,2,3,0,1:T(8,128)S(1)}, f32[4,1,16,2,128]{4,2,3,0,1:T(8,128)S(1)}, u32[]{:S(2)}, u32[]{:S(2)}) collective-permute-start(f32[4,1,16,2,128]{4,2,3,0,1:T(8,128)S(1)} %bitcast.323), channel_id=1, source_target_pairs={{0,16},{2,18},{4,20},{6,22},{8,24},{10,26},{12,28},{14,30},{16,0},... | collective-permute-start | bytes 196616 | tf_op jit(solution)/shard_map/ppermute | solution.py:31
  201.4 13.0 %collective-permute-start.23 = (f32[4,1,16,2,128]{4,2,3,0,1:T(8,128)S(1)}, f32[4,1,16,2,128]{4,2,3,0,1:T(8,128)S(1)}, u32[]{:S(2)}, u32[]{:S(2)}) collective-permute-start(f32[4,1,16,2,128]{4,2,3,0,1:T(8,128)S(1)} %bitcast.321), channel_id=1, source_target_pairs={{0,18},{2,16},{4,22},{6,20},{8,26},{10,24},{12,30},{14,28},{16,2},... | collective-permute-start | bytes 196616 | tf_op jit(solution)/shard_map/ppermute | solution.py:31
  201.8 14.6 %collective-permute-start.24 = (f32[4,1,16,2,128]{4,2,3,0,1:T(8,128)S(1)}, f32[4,1,16,2,128]{4,2,3,0,1:T(8,128)S(1)}, u32[]{:S(2)}, u32[]{:S(2)}) collective-permute-start(f32[4,1,16,2,128]{4,2,3,0,1:T(8,128)S(1)} %bitcast.319), channel_id=1, source_target_pairs={{0,20},{2,22},{4,16},{6,18},{8,28},{10,30},{12,24},{14,26},{16,4},... | collective-permute-start | bytes 196616 | tf_op jit(solution)/shard_map/ppermute | solution.py:31
  203.8 14.9 %collective-permute-start.25 = (f32[4,1,16,2,128]{4,2,3,0,1:T(8,128)S(1)}, f32[4,1,16,2,128]{4,2,3,0,1:T(8,128)S(1)}, u32[]{:S(2)}, u32[]{:S(2)}) collective-permute-start(f32[4,1,16,2,128]{4,2,3,0,1:T(8,128)S(1)} %bitcast.317), channel_id=1, source_target_pairs={{0,22},{2,20},{4,18},{6,16},{8,30},{10,28},{12,26},{14,24},{16,6},... | collective-permute-start | bytes 196616 | tf_op jit(solution)/shard_map/ppermute | solution.py:31
  205.4 13.3 %collective-permute-start.26 = (f32[4,1,16,2,128]{4,2,3,0,1:T(8,128)S(1)}, f32[4,1,16,2,128]{4,2,3,0,1:T(8,128)S(1)}, u32[]{:S(2)}, u32[]{:S(2)}) collective-permute-start(f32[4,1,16,2,128]{4,2,3,0,1:T(8,128)S(1)} %bitcast.315), channel_id=1, source_target_pairs={{0,24},{2,26},{4,28},{6,30},{8,16},{10,18},{12,20},{14,22},{16,8},... | collective-permute-start | bytes 196616 | tf_op jit(solution)/shard_map/ppermute | solution.py:31
  207.5 11.3 %collective-permute-start.27 = (f32[4,1,16,2,128]{4,2,3,0,1:T(8,128)S(1)}, f32[4,1,16,2,128]{4,2,3,0,1:T(8,128)S(1)}, u32[]{:S(2)}, u32[]{:S(2)}) collective-permute-start(f32[4,1,16,2,128]{4,2,3,0,1:T(8,128)S(1)} %bitcast.313), channel_id=1, source_target_pairs={{0,26},{2,24},{4,30},{6,28},{8,18},{10,16},{12,22},{14,20},{16,10}... | collective-permute-start | bytes 196616 | tf_op jit(solution)/shard_map/ppermute | solution.py:31
  214.4 7.0 %collective-permute-start.28 = (f32[4,1,16,2,128]{4,2,3,0,1:T(8,128)S(1)}, f32[4,1,16,2,128]{4,2,3,0,1:T(8,128)S(1)}, u32[]{:S(2)}, u32[]{:S(2)}) collective-permute-start(f32[4,1,16,2,128]{4,2,3,0,1:T(8,128)S(1)} %bitcast.311), channel_id=1, source_target_pairs={{0,28},{2,30},{4,24},{6,26},{8,20},{10,22},{12,16},{14,18},{16,12}... | collective-permute-start | bytes 196616 | tf_op jit(solution)/shard_map/ppermute | solution.py:31
  216.5 7.1 %collective-permute-start.29 = (f32[4,1,16,2,128]{4,2,3,0,1:T(8,128)S(1)}, f32[4,1,16,2,128]{4,2,3,0,1:T(8,128)S(1)}, u32[]{:S(2)}, u32[]{:S(2)}) collective-permute-start(f32[4,1,16,2,128]{4,2,3,0,1:T(8,128)S(1)} %bitcast.309), channel_id=1, source_target_pairs={{0,30},{2,28},{4,26},{6,24},{8,22},{10,20},{12,18},{14,16},{16,14}... | collective-permute-start | bytes 196616 | tf_op jit(solution)/shard_map/ppermute | solution.py:31
  225.2 17.7 %all-to-all-start.9 = ((f32[64,1,16,2,128]{4,2,1,0,3:T(8,128)}), f32[64,1,16,2,128]{4,2,1,0,3:T(8,128)S(1)}, u32[]{:S(2)}, u32[]{:S(2)}) async-start(f32[64,1,16,2,128]{4,2,1,0,3:T(8,128)} %copy.138), calls=%async_computation.9 | async-start | bytes 2097152 | tf_op jit(solution)/shard_map/all_to_all | solution.py:181
  (16 other events, 180.4 us)
